TPU v7x, 32 devices: a whole 2x2x4 slice. The times are simulated.
32 devices in a mesh: zero: 4 (over z), tp: 4 (over x, core), shift: 2 (over y).
Axes of the slice: x: 2, y: 2, z: 4, core: 2. Of those that a mesh axis runs over, the one named last changes fastest.
Arguments:
- train_gate: bfloat16 [4096, 8192], P(('shift', 'zero'), 'tp'), parts along dimension 0, may hold values from -0.125 to 0.125
- low_gate: bfloat16 [4096, 32], P(('shift', 'zero')), parts along dimension 0, may hold values from -0.125 to 0.125
- high_gate: bfloat16 [64, 8192], P('shift', 'tp'), parts along dimension 0, may hold values from -1 to 1
- train_up: bfloat16 [4096, 8192], P(('shift', 'zero'), 'tp'), parts along dimension 0, may hold values from -0.125 to 0.125
- low_up: bfloat16 [4096, 32], P(('shift', 'zero')), parts along dimension 0, may hold values from -0.125 to 0.125
- high_up: bfloat16 [64, 8192], P('shift', 'tp'), parts along dimension 0, may hold values from -1 to 1
- norm_train: float32 [4096], P(('shift', 'zero', 'tp')), parts along dimension 0, may hold values from 0.25 to 1.75
- norm_step: float32 [4096], P(('shift', 'zero', 'tp')), parts along dimension 0, may hold values from -0.3 to 0.3
Outputs:
- ready_gate: bfloat16 [16384, 2048], P(('shift', 'tp')), parts along dimension 0
- ready_up: bfloat16 [16384, 2048], P(('shift', 'tp')), parts along dimension 0
- serve_norm: bfloat16 [4096], P('shift'), parts along dimension 0
There are 2 independent parts, one for each index of `shift`. A program takes and returns all parts, laid end to end along the dimension named above; each array names one. Nothing has to cross between parts.
All inputs are finite; a program needn't handle non-finite values.
Results may differ from a plain program's by a relative error of at most 0.001.
Values may be sent and summed in bfloat16 or wider, within the bound.
A program may use at most 64 MiB of HBM per device.

v0:
```python
import jax
import jax.numpy as jnp
from jax import lax
from jax.sharding import PartitionSpec as P

mix_rate = 0.5


def body(train_gate, low_gate, high_gate, train_up, low_up, high_up, norm_train, norm_step):
    latest_gate = train_gate.astype(jnp.float32) + mix_rate * jnp.dot(
        low_gate, high_gate, preferred_element_type=jnp.float32
    )
    latest_up = train_up.astype(jnp.float32) + mix_rate * jnp.dot(
        low_up, high_up, preferred_element_type=jnp.float32
    )
    narrow_gate, narrow_up = (latest_gate.astype(jnp.bfloat16), latest_up.astype(jnp.bfloat16))
    ready_gate, ready_up = (
        lax.all_gather(narrow_gate, "zero", axis=0, tiled=True),
        lax.all_gather(narrow_up, "zero", axis=0, tiled=True),
    )
    ready_gate, ready_up = (ready_gate.T, ready_up.T)
    serve_norm = lax.all_gather(
        (norm_train + norm_step).astype(jnp.bfloat16), ("zero", "tp"), axis=0, tiled=True
    )
    return (ready_gate, ready_up, serve_norm)


def solution(mesh):
    in_specs = (
        P(("shift", "zero"), "tp"),
        P(("shift", "zero"), None),
        P("shift", "tp"),
        P(("shift", "zero"), "tp"),
        P(("shift", "zero"), None),
        P("shift", "tp"),
        P(("shift", "zero", "tp")),
        P(("shift", "zero", "tp")),
    )
    out_specs = (P(("shift", "tp"), None), P(("shift", "tp"), None), P("shift"))
    return jax.shard_map(body, mesh=mesh, in_specs=in_specs, out_specs=out_specs, check_vma=False)
```

profile of v0, /device:TPU:0, one launch (start us, length us, event | category | flops | bytes accessed | tf_op | source)
XLA Modules:
  0.0 332.7 jit_solution(4366362364971424566)
XLA Ops:
  7.2 0.0 copy-start
  7.2 0.0 copy-start.1
  7.2 0.0 copy-start.3
  7.2 0.0 copy-start.2
  7.2 0.0 all-gather.4.cloned.1.call-start
  7.3 0.8 copy-done
  8.1 3.7 %add_convert_fusion.1 = bf16[512,2048]{1,0:T(8,128)(2,1)} fusion(bf16[512,2048]{1,0:T(8,128)(2,1)} %param.8, bf16[512,32]{0,1:T(8,128)(2,1)} %param.9, bf16[32,2048]{1,0:T(8,128)(2,1)S(1)} %copy-done), kind=kOutput, calls=%fused_computation.1 | convolution fusion | flops 71303168 | bytes 4358144 | tf_op jit(solution)/shard_map/dot_general | solution.py:10
  11.7 0.0 copy-start.4
  11.7 0.0 copy-start.5
  11.7 0.0 all-gather.4.cloned.1.call-update
  11.8 0.0 all-gather.6.cloned.1.call-start
  11.8 0.0 copy-done.1
  11.8 0.0 copy-done.3
  11.8 0.0 copy-done.2
  11.8 2.1 add_convert_fusion
  13.9 0.0 all-gather.6.cloned.1.call-update
  13.9 0.0 copy-done.4
  13.9 0.0 copy-done.5
  14.0 23.5 %all-gather = bf16[16,1,128]{2,1,0:T(2,128)(2,1)S(1)} all-gather(bf16[1,1,128]{2,1,0:T(2,128)(2,1)S(1)} %convert_bitcast_fusion), channel_id=1, replica_groups=mesh['zero'=4,'tp'=4,'shift'=2] {'zero','tp'}, dimensions={0}, use_global_device_ids=true | all-gather | bytes 4352 | tf_op jit(solution)/shard_map/all_gather | solution.py:22
  37.5 0.6 reduce
  38.1 126.2 %all-gather.4.cloned.1.call-done = bf16[2048,2048]{1,0:T(8,128)(2,1)} async-done(((bf16[512,2048]{1,0:T(8,128)(2,1)}), bf16[2048,2048]{1,0:T(8,128)(2,1)}) %all-gather.4.cloned.1.call-update) | async-done | bytes 8388624 | tf_op jit(solution)/shard_map/all_gather | solution.py:18
  164.3 12.4 %copy.15 = bf16[2048,2048]{1,0:T(8,128)(2,1)} copy(bf16[2048,2048]{0,1:T(8,128)(2,1)} %bitcast.9) | data formatting | bytes 16777216
  176.7 137.0 %all-gather.6.cloned.1.call-done = bf16[2048,2048]{1,0:T(8,128)(2,1)} async-done(((bf16[512,2048]{1,0:T(8,128)(2,1)}), bf16[2048,2048]{1,0:T(8,128)(2,1)}) %all-gather.6.cloned.1.call-update) | async-done | bytes 8388624 | tf_op jit(solution)/shard_map/all_gather | solution.py:19
  313.7 12.2 %copy.16 = bf16[2048,2048]{1,0:T(8,128)(2,1)} copy(bf16[2048,2048]{0,1:T(8,128)(2,1)} %bitcast.10) | data formatting | bytes 16777216
  (1 shorter events, 0.0 us)
Async XLA Ops:
  7.2 0.9 copy-start
  7.2 4.6 %copy-start.1 = (bf16[512,2048]{1,0:T(8,128)(2,1)S(1)}, bf16[512,2048]{1,0:T(8,128)(2,1)}, u32[]{:S(2)}) copy-start(bf16[512,2048]{1,0:T(8,128)(2,1)} %param.11) | copy-start | bytes 6291460
  7.2 4.6 %copy-start.3 = (bf16[512,32]{0,1:T(8,128)(2,1)S(1)}, bf16[512,32]{0,1:T(8,128)(2,1)}, u32[]{:S(2)}) copy-start(bf16[512,32]{0,1:T(8,128)(2,1)} %param.12) | copy-start | bytes 98308
  7.2 4.6 %copy-start.2 = (bf16[32,2048]{1,0:T(8,128)(2,1)S(1)}, bf16[32,2048]{1,0:T(8,128)(2,1)}, u32[]{:S(2)}) copy-start(bf16[32,2048]{1,0:T(8,128)(2,1)} %param.13) | copy-start | bytes 393220
  7.2 157.0 %all-gather.4.cloned.1.call-start = ((), (), s32[]{:S(2)}) async-start(), calls=%async_computation | async-start | bytes 10485760 | tf_op jit(solution)/shard_map/all_gather | solution.py:18
  11.7 2.2 copy-start.4
  11.7 2.2 copy-start.5
  11.8 301.9 %all-gather.6.cloned.1.call-start = ((), (), s32[]{:S(2)}) async-start(), calls=%async_computation.1 | async-start | bytes 10485760 | tf_op jit(solution)/shard_map/all_gather | solution.py:19
Sparse Core Ops, SparseCore 0:
  11.9 152.3 all-gather.3
  165.8 147.8 all-gather.5
where the time goes:
time: 333 us
  waiting for transfers between devices  263 us (79%)
  local copies, waits for them, and re-layouts  25.5 us (8%)
  blocking collectives  23.5 us (7%)
  between operations  14.1 us (4%)
  matrix products  5.73 us (2%)
    all_gather x1, waiting for transfers between devices, body(): lax.all_gather(narrow_up, 'zero', axis=0, tiled=True)  137 us
    all_gather x1, waiting for transfers between devices, body(): lax.all_gather(narrow_gate, 'zero', axis=0, tiled=True)  126 us
    unnamed x14, local copies, waits for them, and re-layouts  25.5 us
    all_gather x1, blocking collectives, body(): lax.all_gather((norm_train + norm_step).astype(jnp.bfloat16), ('zero', 't...  23.5 us
  transfers between devices with their start and end apart: 2, of which 2 were waited for; matrix products, arithmetic and copies ran while one was open for 5% of the time, Pallas kernels for 0%

commit v1 on v0

--- a/solution.py
+++ b/solution.py
@@ -15,7 +15,9 @@
     )
     narrow_gate, narrow_up = (latest_gate.astype(jnp.bfloat16), latest_up.astype(jnp.bfloat16))
     ready_gate, ready_up = (
-        lax.all_gather(narrow_gate, "zero", axis=0, tiled=True),
+        jnp.concatenate(
+            lax.all_to_all(jnp.stack([narrow_gate] * lax.axis_size("zero")), "zero", 0, 0), axis=0
+        ),
         lax.all_gather(narrow_up, "zero", axis=0, tiled=True),
     )
     ready_gate, ready_up = (ready_gate.T, ready_up.T)

time: 333 us -> 396 us (1.19)
  the two profiles are of different devices: /device:TPU:0 before, /device:TPU:13 now
where the time goes in v1:
time: 396 us; the launch traced here: 395 us
  blocking collectives  325 us (82%)
  local copies, waits for them, and re-layouts  43.6 us (11%)
  between operations  14.1 us (4%)
  starting transfers between devices  5.9 us (1%)
  matrix products  5.74 us (1%)
    all_gather x1, blocking collectives, body(): lax.all_gather((norm_train + norm_step).astype(jnp.bfloat16), ('zero', 't...  325 us
    unnamed x14, local copies, waits for them, and re-layouts  25.4 us
    all_to_all x1, local copies, waits for them, and re-layouts, body(): lax.all_to_all(jnp.stack([narrow_gate] * lax.axis_size('zero')), 'zero',...  11.3 us
  transfers between devices with their start and end apart: 2, of which 0 were waited for; matrix products, arithmetic and copies ran while one was open for 7% of the time, Pallas kernels for 0%

profile of v1, /device:TPU:13, one launch (start us, length us, event | category | flops | bytes accessed | tf_op | source)
XLA Modules:
  0.0 395.1 jit_solution(9445103498093579790)
XLA Ops:
  7.2 0.0 copy-start
  7.2 0.9 copy-done
  8.1 3.7 add_convert_fusion.1
  11.7 2.9 copy.17
  14.6 4.1 %stack.2 = bf16[4,512,2048]{1,2,0:T(8,128)(2,1)} broadcast(bf16[512,2048]{0,1:T(8,128)(2,1)S(1)} %copy.17), dimensions={1,2} | broadcast | bytes 10485760 | tf_op jit(solution)/shard_map/stack | solution.py:19
  18.7 0.0 copy-start.1
  18.7 0.0 copy-start.2
  18.7 0.0 copy-start.3
  18.7 5.9 %all-to-all-start = ((bf16[4,512,2048]{1,2,0:T(8,128)(2,1)}), bf16[4,512,2048]{1,2,0:T(8,128)(2,1)}, u32[]{:S(2)}, u32[]{:S(2)}) async-start(bf16[4,512,2048]{1,2,0:T(8,128)(2,1)} %stack.2), calls=%async_computation | async-start | bytes 16777216 | tf_op jit(solution)/shard_map/all_to_all | solution.py:19
  24.6 0.0 copy-start.4
  24.6 0.0 all-gather.3.cloned.1.call-start
  24.6 0.0 copy-done.1
  24.6 0.0 copy-done.2
  24.6 0.0 copy-done.3
  24.6 2.1 add_convert_fusion
  26.7 0.0 all-gather.3.cloned.1.call-update
  26.7 0.0 copy-done.4
  26.7 0.0 copy-done.5
  26.7 325.1 %all-gather = bf16[16,1,128]{2,1,0:T(2,128)(2,1)S(1)} all-gather(bf16[1,1,128]{2,1,0:T(2,128)(2,1)S(1)} %convert_bitcast_fusion), channel_id=1, replica_groups=mesh['zero'=4,'tp'=4,'shift'=2] {'zero','tp'}, dimensions={0}, use_global_device_ids=true | all-gather | bytes 4352 | tf_op jit(solution)/shard_map/all_gather | solution.py:24
  351.9 0.6 reduce
  352.5 0.0 all-to-all-done
  352.5 11.3 %copy.18 = bf16[4,512,2048]{2,1,0:T(8,128)(2,1)} copy(bf16[4,512,2048]{1,2,0:T(8,128)(2,1)} %all-to-all-done) | data formatting | bytes 16777216 | tf_op jit(solution)/shard_map/all_to_all | solution.py:19
  363.8 12.2 %copy.19 = bf16[2048,2048]{1,0:T(8,128)(2,1)} copy(bf16[2048,2048]{0,1:T(8,128)(2,1)} %bitcast.11) | data formatting | bytes 16777216
  376.1 12.2 %copy.20 = bf16[2048,2048]{1,0:T(8,128)(2,1)} copy(bf16[2048,2048]{0,1:T(8,128)(2,1)} %bitcast.12) | data formatting | bytes 16777216
  (3 shorter events, 0.0 us)
Async XLA Ops:
  7.2 0.9 copy-start
  18.7 5.9 %copy-start.1 = (bf16[512,2048]{1,0:T(8,128)(2,1)S(1)}, bf16[512,2048]{1,0:T(8,128)(2,1)}, u32[]{:S(2)}) copy-start(bf16[512,2048]{1,0:T(8,128)(2,1)} %param.11) | copy-start | bytes 6291460
  18.7 5.9 %copy-start.2 = (bf16[32,2048]{1,0:T(8,128)(2,1)S(1)}, bf16[32,2048]{1,0:T(8,128)(2,1)}, u32[]{:S(2)}) copy-start(bf16[32,2048]{1,0:T(8,128)(2,1)} %param.13) | copy-start | bytes 393220
  18.7 5.9 %copy-start.3 = (bf16[512,32]{0,1:T(8,128)(2,1)S(1)}, bf16[512,32]{0,1:T(8,128)(2,1)}, u32[]{:S(2)}) copy-start(bf16[512,32]{0,1:T(8,128)(2,1)} %param.12) | copy-start | bytes 98308
  18.7 333.8 %all-to-all-start = ((bf16[4,512,2048]{1,2,0:T(8,128)(2,1)}), bf16[4,512,2048]{1,2,0:T(8,128)(2,1)}, u32[]{:S(2)}, u32[]{:S(2)}) async-start(bf16[4,512,2048]{1,2,0:T(8,128)(2,1)} %stack.2), calls=%async_computation | async-start | bytes 16777216 | tf_op jit(solution)/shard_map/all_to_all | solution.py:19
  24.6 2.1 copy-start.4
  24.6 2.1 copy-start.5
  24.6 351.5 %all-gather.3.cloned.1.call-start = ((), (), s32[]{:S(2)}) async-start(), calls=%async_computation.1 | async-start | bytes 10485760 | tf_op jit(solution)/shard_map/all_gather | solution.py:21
Sparse Core Ops, SparseCore 0:
  26.9 304.4 all-gather.2
